TPU v7x, 128 devices: a whole 4x4x4 slice. The times are simulated.
128 devices in a mesh: half: 2 (over core), vocab: 32 (over y_hi, x, z), tok: 2 (over y_lo).
Axes of the slice: x: 4, y: 4 (y_hi: 2, y_lo: 2; y = y_hi * 2 + y_lo), z: 4, core: 2. Of those that a mesh axis runs over, the one named last changes fastest.
Arguments:
- teacher_hidden: bfloat16 [2048, 8192], P('vocab', ('half', 'tok')), may hold values from -400 to 400
- student_hidden: bfloat16 [2048, 4096], P('vocab', ('half', 'tok')), may hold values from -400 to 400
- teacher_gain: float32 [8192], P(('half', 'tok')), may hold values from 0.5 to 1.5
- student_gain: float32 [4096], P(('half', 'tok')), may hold values from 0.5 to 1.5
- teacher_head: bfloat16 [8192, 65536], P(('half', 'tok'), 'vocab'), may hold values from -1 to 1
- student_head: bfloat16 [4096, 65536], P(('half', 'tok'), 'vocab'), may hold values from -2 to 2
- labels: int32 [2048], P(('half', 'tok')), may hold values from 0 to 65535
Outputs:
- token_loss: float32 [2048], P(('half', 'tok'))
- logit_grad: bfloat16 [2048, 65536], P(('half', 'tok'), 'vocab')
All inputs are finite; a program needn't handle non-finite values.
Results may differ from a plain program's by a relative error of at most 0.0068.
Values may be sent and summed in bfloat16 or wider, within the bound.
A program may use at most 192 MiB of HBM per device.

v0:
```python
import jax
import jax.numpy as jnp
from jax import lax
from jax.sharding import PartitionSpec as P

DT = 8192
DS = 4096


epsilon = 1e-05
label_weight = 0.5


def in_one_piece(arrays, axis, dim, along):
    both = jnp.concatenate(arrays, axis=along)
    out, at, done = (lax.all_gather(both, axis, axis=dim, tiled=True), 0, [])
    for a in arrays:
        done.append(lax.slice_in_dim(out, at, at + a.shape[along], axis=along))
        at += a.shape[along]
    return tuple(done)


def sum_by_axis(value, axes, dim):
    if not axes:
        return value
    nearer = lax.psum_scatter(value, axes[0], scatter_dimension=dim, tiled=True)
    return sum_by_axis(nearer, axes[1:], dim)


def in_one_piece_2(arrays, axis, dim, along):
    columns = [a.reshape(*a.shape[:along], -1) for a in arrays]
    both = jnp.concatenate(columns, axis=along)
    out, at, done = (lax.psum_scatter(both, axis, scatter_dimension=dim, tiled=True), 0, [])
    for a, column in zip(arrays, columns):
        section = out[..., at : at + column.shape[along]]
        done.append(section.reshape(*section.shape[:along], *a.shape[along:]))
        at += column.shape[along]
    return tuple(done)


def sent_to_all(value, axis):
    copies = jnp.broadcast_to(value, (lax.axis_size(axis), *value.shape))
    return lax.all_to_all(copies, axis, split_axis=0, concat_axis=0, tiled=True)


def collected_together(value, axis):
    leaves = jax.tree.leaves(value)
    turns = sorted(range(len(leaves)), key=lambda k: -leaves[k].size)
    width = (1, *leaves[turns[0]].shape)[-1]
    lines = [
        jnp.pad(leaves[k].reshape(-1), (0, -leaves[k].size % width)).reshape(-1, width)
        for k in turns
    ]
    both, at, found = (sent_to_all(jnp.concatenate(lines), axis), 0, {})
    for k, line in zip(turns, lines):
        section = both[:, at : at + len(line)].reshape(len(both), -1)
        found[k] = section[:, : leaves[k].size].reshape(-1, *leaves[k].shape)
        at += len(line)
    numbers = iter(range(len(leaves)))
    return jax.tree.map(lambda _: found[next(numbers)], value)


def joined_by_halves(pieces, combine):
    while len(jax.tree.leaves(pieces)[0]) > 1:
        pieces = jax.vmap(combine)(
            *(jax.tree.map(lambda part: part[side::2], pieces) for side in (0, 1))
        )
    return jax.tree.map(lambda part: part[0], pieces)


def combined_all(value, axis, combine):
    pieces = collected_together(value, axis)
    return joined_by_halves(pieces, combine)


def prepare(rows, gain):
    values = rows.astype(jnp.float32)
    squares = jnp.sum(values * values, axis=1)
    scaled = (values * gain[None, :]).astype(jnp.bfloat16)
    return (scaled, squares)


def combine_stats(first, second):
    t_max1, t_tot1, cross1, s_max1, s_tot1, target1 = first
    t_max2, t_tot2, cross2, s_max2, s_tot2, target2 = second
    t_max = jnp.maximum(t_max1, t_max2)
    t_one = jnp.exp(t_max1 - t_max)
    t_two = jnp.exp(t_max2 - t_max)
    s_max = jnp.maximum(s_max1, s_max2)
    s_one = jnp.exp(s_max1 - s_max)
    s_two = jnp.exp(s_max2 - s_max)
    return (
        t_max,
        t_tot1 * t_one + t_tot2 * t_two,
        cross1 * t_one + cross2 * t_two,
        s_max,
        s_tot1 * s_one + s_tot2 * s_two,
        target1 + target2,
    )


def shards(
    teacher_hidden, student_hidden, teacher_gain, student_gain, teacher_head, student_head, labels
):
    gathered_t, gathered_s = in_one_piece((teacher_hidden, student_hidden), "vocab", 0, 1)
    scaled_t, squares_t = prepare(gathered_t, teacher_gain)
    scaled_s, squares_s = prepare(gathered_s, student_gain)
    partial_t = jnp.dot(scaled_t, teacher_head, preferred_element_type=jnp.float32)
    owned_t, summed_t = (
        sum_by_axis(partial_t, ("half", "tok"), 0),
        sum_by_axis(squares_t, ("half", "tok"), 0),
    )
    partial_s = jnp.dot(scaled_s, student_head, preferred_element_type=jnp.float32)
    owned_s, summed_s = in_one_piece_2((partial_s, squares_s), ("half", "tok"), 0, 1)
    teacher_logits = owned_t * lax.rsqrt(summed_t / DT + epsilon)[:, None]
    student_logits = owned_s * lax.rsqrt(summed_s / DS + epsilon)[:, None]
    width_here = teacher_logits.shape[1]
    columns = (
        lax.broadcasted_iota(jnp.int32, teacher_logits.shape, 1)
        + lax.axis_index("vocab") * width_here
    )
    is_label = columns == labels[:, None]
    label_terms = jnp.where(is_label, student_logits, jnp.float32(0.0))
    local_t = jnp.max(teacher_logits, axis=1)
    local_s = jnp.max(student_logits, axis=1)
    exp_t = jnp.exp(teacher_logits - local_t[:, None])
    exp_s = jnp.exp(student_logits - local_s[:, None])
    teacher_max, teacher_total, cross, student_max, student_total, target = combined_all(
        (
            local_t,
            jnp.sum(exp_t, axis=1),
            jnp.sum(exp_t * (teacher_logits - student_logits), axis=1),
            local_s,
            jnp.sum(exp_s, axis=1),
            jnp.sum(label_terms, axis=1),
        ),
        "vocab",
        combine_stats,
    )
    teacher_prob = exp_t * (jnp.exp(local_t - teacher_max) / teacher_total)[:, None]
    student_prob = exp_s * (jnp.exp(local_s - student_max) / student_total)[:, None]
    student_lse = student_max + jnp.log(student_total)
    token_loss = (
        cross / teacher_total
        - teacher_max
        - jnp.log(teacher_total)
        + student_lse
        + label_weight * (student_lse - target)
    )
    logit_grad = (
        (1.0 + label_weight) * student_prob
        - teacher_prob
        - label_weight * is_label.astype(jnp.float32)
    )
    return (token_loss, logit_grad.astype(jnp.bfloat16))


def solution(mesh):
    return jax.shard_map(
        shards,
        mesh=mesh,
        in_specs=(
            P("vocab", ("half", "tok")),
            P("vocab", ("half", "tok")),
            P(("half", "tok")),
            P(("half", "tok")),
            P(("half", "tok"), "vocab"),
            P(("half", "tok"), "vocab"),
            P(("half", "tok")),
        ),
        out_specs=(P(("half", "tok")), P(("half", "tok"), "vocab")),
        check_vma=False,
    )
```

profile of v0, /device:TPU:0, one launch (start us, length us, event | category | flops | bytes accessed | tf_op | source)
XLA Modules:
  0.0 645.0 jit_solution(6338925652752829093)
XLA Ops:
  7.2 0.0 all-gather.2.cloned.1.call-start
  7.2 1.8 pad_maximum_fusion.1
  9.0 0.0 all-gather.2.cloned.1.call-update
  9.0 0.0 reduce-scatter.4.cloned.1.call-start
  9.1 133.7 %all-gather.2.cloned.1.call-done = bf16[2048,3072]{1,0:T(8,128)(2,1)} async-done(((bf16[64,3072]{1,0:T(8,128)(2,1)}), bf16[2048,3072]{1,0:T(8,128)(2,1)}) %all-gather.2.cloned.1.call-update) | async-done | bytes 12582928 | tf_op jit(solution)/shard_map/all_gather | solution.py:16
  142.8 24.0 %fusion.4 = f32[2048,2048]{1,0:T(8,128)} fusion(bf16[2048,2048]{1,0:T(8,128)(2,1)} %param.11, f32[2048]{0:T(1024)} %param.9, bf16[2048,3072]{1,0:T(8,128)(2,1)} %all-gather.2.cloned.1.call-done), kind=kOutput, calls=%fused_computation.9 | convolution fusion | flops 17192452096 | bytes 33562624 | tf_op jit(solution)/shard_map/dot_general | solution.py:108
  166.8 0.0 reduce-scatter.4.cloned.1.call-update
  166.9 0.0 copy-start.2
  166.9 0.0 reduce-scatter.8.cloned.1.call-start
  166.9 3.1 fusion.3
  170.0 0.4 copy.19
  170.4 0.0 copy-done.2
  170.4 11.9 %fusion.11 = f32[2048,2048]{1,0:T(8,128)S(1)} fusion(bf16[1024,2048]{1,0:T(8,128)(2,1)} %param.12, f32[1024]{0:T(1024)S(1)} %copy-done.2, bf16[2048,3072]{1,0:T(8,128)(2,1)} %all-gather.2.cloned.1.call-done), kind=kOutput, calls=%fused_computation.17 | convolution fusion | flops 8596226048 | bytes 25169920 | tf_op jit(solution)/shard_map/dot_general | solution.py:113
  182.2 10.0 %pad_maximum_fusion = f32[2048,2049]{1,0:T(8,128)} fusion(f32[2048,1]{1,0:T(8,128)S(1)} %copy.19, f32[2048,2048]{1,0:T(8,128)S(1)} %fusion.11), kind=kLoop, calls=%fused_computation.2 | loop fusion | flops 4196352 | bytes 33570816 | tf_op jit(solution)/shard_map/concatenate | solution.py:32
  192.3 0.0 reduce-scatter.8.cloned.1.call-update
  192.3 0.0 reduce-scatter.6.cloned.1.call-start
  192.3 0.2 reduce-scatter.4.cloned.1.call-done
  192.5 0.0 copy-start.4
  192.6 0.0 copy-start.3
  192.6 0.3 reduce-scatter.6.cloned.1.call-update
  192.9 0.3 copy-done.4
  193.2 0.6 dynamic-slice
  193.8 0.0 copy-done.3
  193.8 0.6 dynamic-slice.2
  195.7 5.1 fusion.1
  200.8 0.0 copy-start.1
  200.8 2.5 all-reduce
  203.3 4.9 all-reduce.1
  208.2 0.1 fusion.25
  208.3 286.7 %reduce-scatter.8.cloned.1.call-done = f32[512,2049]{1,0:T(8,128)} async-done(((f32[2048,2049]{1,0:T(8,128)}), f32[512,2049]{1,0:T(8,128)}) %reduce-scatter.8.cloned.1.call-update) | async-done | bytes 4196368 | tf_op jit(solution)/shard_map/reduce_scatter | solution.py:33
  495.0 1.1 fusion.20
  496.1 104.0 %reduce-scatter.6.cloned.1.call-done = f32[512,2048]{1,0:T(8,128)} async-done(((f32[1024,2048]{1,0:T(8,128)}), f32[512,2048]{1,0:T(8,128)}) %reduce-scatter.6.cloned.1.call-update) | async-done | bytes 4194320 | tf_op jit(solution)/shard_map/reduce_scatter | solution.py:26
  600.1 0.0 copy-start
  600.1 0.0 slice-start
  600.1 2.8 multiply_reduce_fusion.1
  602.8 0.0 copy-done.1
  602.8 0.7 copy-done
  603.5 0.0 slice-start.1
  603.5 4.0 fusion.8
  607.5 0.0 slice-done
  607.5 0.0 slice-done.1
  607.5 0.8 fusion.15
  608.4 0.1 broadcast_in_dim.7
  608.5 22.0 %all_to_all.5 = f32[32,6,512]{2,1,0:T(8,128)S(1)} all-to-all(f32[32,6,512]{2,1,0:T(8,128)S(1)} %broadcast_in_dim.7), channel_id=1, replica_groups=mesh['half'=2,'vocab'=32,'tok'=2] {'vocab'}, dimensions={0} | all-to-all | bytes 786432 | tf_op jit(solution)/shard_map/all_to_all | solution.py:43
  630.5 0.3 fusion.26
  632.3 0.6 exponential_divide_fusion.1
  632.9 5.6 fusion.10
  (75 shorter events, 1.4 us)
Async XLA Ops:
  7.2 135.7 %all-gather.2.cloned.1.call-start = ((), (), s32[]{:S(2)}) async-start(), calls=%async_computation.4 | async-start | bytes 12976128 | tf_op jit(solution)/shard_map/all_gather | solution.py:16
  9.0 183.5 %reduce-scatter.4.cloned.1.call-start = ((), (), s32[]{:S(2)}) async-start(), calls=%async_computation.5 | async-start | bytes 25165824 | tf_op jit(solution)/shard_map/reduce_scatter | solution.py:26
  166.9 3.5 copy-start.2
  166.9 328.1 %reduce-scatter.8.cloned.1.call-start = ((), (), s32[]{:S(2)}) async-start(), calls=%async_computation.7 | async-start | bytes 22282240 | tf_op jit(solution)/shard_map/reduce_scatter | solution.py:33
  192.3 407.8 %reduce-scatter.6.cloned.1.call-start = ((), (), s32[]{:S(2)}) async-start(), calls=%async_computation.6 | async-start | bytes 12582912 | tf_op jit(solution)/shard_map/reduce_scatter | solution.py:26
  192.5 0.7 copy-start.4
  192.6 1.2 copy-start.3
  200.8 402.1 %copy-start.1 = (s32[512]{0:T(512)S(1)}, s32[512]{0:T(512)}, u32[]{:S(2)}) copy-start(s32[512]{0:T(512)} %param.13) | copy-start | bytes 6148
  600.1 3.4 copy-start
  600.1 7.4 %slice-start = ((s8[4456448]{0:T(1024)(128)(4,1)}), s8[4194304]{0:T(1024)(128)(4,1)S(1)}, s32[]{:S(2)}) async-start(s8[4456448]{0:T(1024)(128)(4,1)} %bitcast.29), calls=%async_computation.8 | async-start | bytes 8388608
  603.5 4.0 slice-start.1
Sparse Core Ops, SparseCore 0:
  11.6 131.1 all-gather.1
  167.0 25.5 reduce-scatter.3
  195.0 299.8 reduce-scatter.7
  497.2 102.7 reduce-scatter.5
where the time goes:
time: 645 us
  waiting for transfers between devices  525 us (81%)
  matrix products  35.9 us (6%)
  other arithmetic  35.3 us (5%)
  blocking collectives  29.5 us (5%)
  between operations  15.3 us (2%)
    reduce_scatter x1, waiting for transfers between devices, in_one_piece_2(): lax.psum_scatter(both, axis, scatter_dimension=dim, tiled=True)  287 us
    all_gather x1, waiting for transfers between devices, in_one_piece(): out, at, done = (lax.all_gather(both, axis, axis=dim, tiled=True), 0, [])  134 us
    reduce_scatter x2, waiting for transfers between devices, sum_by_axis(): nearer = lax.psum_scatter(value, axes[0], scatter_dimension=dim, tiled=True)  104 us
    dot_general x1, matrix products, shards(): jnp.dot(scaled_t, teacher_head, preferred_element_type=jnp.float32)  24 us
    all_to_all x1, blocking collectives, sent_to_all(): return lax.all_to_all(copies, axis, split_axis=0, concat_axis=0, tiled=True)  22 us
  transfers between devices with their start and end apart: 4, of which 4 were waited for; matrix products, arithmetic and copies ran while one was open for 5% of the time, Pallas kernels for 0%

commit v1 on v0

v1 whole, which is shorter than its diff:
```python
import jax
import jax.numpy as jnp
from jax import lax
from jax.experimental import pallas as pl
from jax.experimental.pallas import tpu as pltpu
from jax.sharding import PartitionSpec as P

DT = 8192
DS = 4096
EPS = 1e-05
LABEL_WEIGHT = 0.5

N = 4
ROWS = 64
MINE = 512
WIDE = 2048
COLS = 512
TILES = WIDE // COLS
PART = 64
FULL = 32000.0

f32 = jnp.float32
bf16 = jnp.bfloat16
i16 = jnp.int16
MESH = pl.DeviceIdType.MESH


def remote(src, dst, send, recv, where):
    return pltpu.make_async_remote_copy(
        src_ref=src, dst_ref=dst, send_sem=send, recv_sem=recv, device_id=where, device_id_type=MESH
    )


def turned(row):
    return jnp.transpose(jnp.concatenate([row] * 16, axis=0))


def joined(a, b):
    t_max = jnp.maximum(a[0:1], b[0:1])
    t_a, t_b = jnp.exp(a[0:1] - t_max), jnp.exp(b[0:1] - t_max)
    s_max = jnp.maximum(a[3:4], b[3:4])
    s_a, s_b = jnp.exp(a[3:4] - s_max), jnp.exp(b[3:4] - s_max)
    return jnp.concatenate(
        [
            t_max,
            a[1:2] * t_a + b[1:2] * t_b,
            a[2:3] * t_a + b[2:3] * t_b,
            s_max,
            a[4:5] * s_a + b[4:5] * s_b,
            a[5:6] + b[5:6],
            a[6:8],
        ],
        axis=0,
    )


def kernel(
    th, sh, gt, gs, lab, wt, ws, loss, grad,
    XS, XT, WS, WT, GS, GT, QS, SQ, INV, NS, NT, ACC, OS, OT, US, UT, RS, RT, OUT,
    MS, LS, TG, MT, LT, CR, STA, STR, FIN,
    x0_send, x0_recv, q_send, q_recv, i_send, i_recv, w_send, w_recv, w_loc,
    r_send, r_recv, e_send, e_recv, s_send, s_recv, o_sem,
):
    h, v, t = lax.axis_index("half"), lax.axis_index("vocab"), lax.axis_index("tok")
    yh = v // 16
    x = (v % 16) // 4
    z = v % 4
    far = (v + 16) % 32
    started = []

    def go(copy):
        copy.start()
        started.append(copy)

    def at(xx, zz):
        return {"half": h, "vocab": yh * 16 + (xx % N) * N + zz % N, "tok": t}

    values_t = th[...].astype(f32)
    values_s = sh[...].astype(f32)
    GT[...] = (values_t * gt[...]).astype(bf16)
    GS[...] = (values_s * gs[...]).astype(bf16)
    squares = jnp.concatenate(
        [
            jnp.sum(values_t * values_t, axis=1, keepdims=True),
            jnp.sum(values_s * values_s, axis=1, keepdims=True),
        ],
        axis=0,
    )
    q = h * 2 + t
    QS[...] = jnp.transpose(jnp.broadcast_to(squares, (128, 128)))[0:8]

    @pl.when(h == yh)
    def _():
        SQ[q] = QS[...]
        XS[h, x, z] = GS[...]
        XT[h, x, z] = GT[...]

    barrier = pltpu.get_barrier_semaphore()
    near = [
        {"half": (h + a) % 2, "vocab": (v + 16 * b) % 32, "tok": (t + c) % 2}
        for a in (0, 1) for b in (0, 1) for c in (0, 1) if a + b + c
    ]
    near += [at(x, z + d) for d in (1, 2, 3)] + [at(x + d, z) for d in (1, 2, 3)]
    for where in near:
        pl.semaphore_signal(barrier, inc=1, device_id=where, device_id_type=MESH)
    pl.semaphore_wait(barrier, len(near))

    sets = ((GS, XS, 0), (GT, XT, 1))

    def first(k, where_far):
        g, X, _ = sets[k]
        return remote(
            g, X.at[h, x, z], x0_send.at[k, int(where_far)], x0_recv.at[k, h],
            {"half": yh, "vocab": far if where_far else v, "tok": t},
        )

    def squares_to(b, c):
        return remote(
            QS, SQ.at[q], q_send.at[2 * b + c], q_recv.at[q],
            {"half": yh, "vocab": (v + 16 * b) % 32, "tok": (t + c) % 2},
        )

    def first_arrived(k, c):
        X = sets[k][1]
        remote(X.at[c, x, z], X.at[c, x, z], x0_send.at[k, 0], x0_recv.at[k, c], near[0]).wait_recv()

    go(first(0, True))

    @pl.when(h != yh)
    def _():
        first(0, False).start()
        squares_to(0, 0).start()
        first(1, False).start()

    for b, c in ((0, 1), (1, 0), (1, 1)):
        go(squares_to(b, c))
    go(first(1, True))

    other = near[3]
    loads = [
        pltpu.make_async_copy(ws, WS.at[h], w_loc.at[0]),
        pltpu.make_async_copy(wt, WT.at[h], w_loc.at[1]),
    ]
    for k, (w, W) in enumerate(((ws, WS), (wt, WT))):
        go(remote(w, W.at[h], w_send.at[k], w_recv.at[k], other))
        loads[k].start()

    def head_here(k):
        W = (WS, WT)[k]
        loads[k].wait()
        remote(W.at[1 - h], W.at[1 - h], w_send.at[k], w_recv.at[k], other).wait_recv()

    def steps(k, c):
        X = sets[k][1]
        half_rows = ROWS // 2

        def block(r, lo=None):
            xx, zz = (x, r % N) if c == 0 else (r % N, z)
            return X.at[c, xx, zz] if lo is None else X.at[c, xx, zz, pl.ds(lo, half_rows)]

        def line(r, lo=None):
            if c == 0:
                return X.at[0, r % N] if lo is None else X.at[0, r % N, pl.ds(lo, 2)]
            return X.at[1, :, r % N] if lo is None else X.at[1, pl.ds(lo, 2), r % N]

        a, b = (z, x) if c == 0 else (x, z)

        def to(phase, d):
            along_z = (phase == 0) == (c == 0)
            return at(x, z + d) if along_z else at(x + d, z)

        def copy(step, ref, where):
            return remote(ref, ref, r_send.at[k, c, step], r_recv.at[k, c, step], where)

        sends = (
            (copy(0, block(a), to(0, 1)), copy(1, block(a), to(0, 3))),
            (copy(2, block(a + 3, 0), to(0, 1)), copy(3, block(a + 1, half_rows), to(0, 3))),
            (copy(4, line(b), to(1, 1)), copy(5, line(b), to(1, 3))),
            (copy(6, line(b + 3, 0), to(1, 1)), copy(7, line(b + 1, 2), to(1, 3))),
        )
        takes = (
            (copy(0, block(a + 3), to(0, 3)), copy(1, block(a + 1), to(0, 1))),
            (copy(2, block(a + 2, 0), to(0, 3)), copy(3, block(a + 2, half_rows), to(0, 1))),
            (copy(4, line(b + 3), to(1, 3)), copy(5, line(b + 1), to(1, 1))),
            (copy(6, line(b + 2, 0), to(1, 3)), copy(7, line(b + 2, 2), to(1, 1))),
        )
        return sends, takes

    plans = [[steps(k, c) for c in (0, 1)] for k in (0, 1)]

    def send(k, step):
        for c in (0, 1):
            for copy in plans[k][c][0][step]:
                go(copy)

    def take(k, step):
        for c in (0, 1):
            for copy in plans[k][c][1][step]:
                copy.wait_recv()

    def first_take(k):
        first_arrived_mine = 1 - h

        @pl.when(h == yh)
        def _():
            first_arrived(k, first_arrived_mine)

        @pl.when(h != yh)
        def _():
            first_arrived(k, 0)
            first_arrived(k, 1)

    first_take(0)
    send(0, 0)

    for j in range(4):
        def arrived(j=j):
            remote(SQ.at[j], SQ.at[j], q_send.at[0], q_recv.at[j], near[0]).wait_recv()

        pl.when(jnp.logical_or(h != yh, q != j))(arrived)
    lane = lax.broadcasted_iota(jnp.int32, (8, 128), 1)
    total = (SQ[0] + SQ[1]) + (SQ[2] + SQ[3])
    INV[x, z] = lax.rsqrt(jnp.where(lane < 64, total / DT, total / DS) + EPS)

    take(0, 0)
    send(0, 1)
    for d in (1, 2, 3):
        go(remote(INV.at[x, z], INV.at[x, z], i_send.at[0, d - 1], i_recv.at[0, d - 1], at(x, z + d)))
    first_take(1)
    send(1, 0)
    take(0, 1)
    send(0, 2)
    for d in (1, 2, 3):
        ref = INV.at[x, (z + N - d) % N]
        remote(ref, ref, i_send.at[0, d - 1], i_recv.at[0, d - 1], at(x, z + N - d)).wait_recv()
    for d in (1, 2, 3):
        go(remote(INV.at[x], INV.at[x], i_send.at[1, d - 1], i_recv.at[1, d - 1], at(x + d, z)))
    take(0, 2)
    send(0, 3)
    take(1, 0)
    send(1, 1)
    for d in (1, 2, 3):
        ref = INV.at[(x + N - d) % N]
        remote(ref, ref, i_send.at[1, d - 1], i_recv.at[1, d - 1], at(x + N - d, z)).wait_recv()
    spread = jnp.transpose(INV[...].reshape(128, 128))
    for j in range(16):
        NT[j // 4, j % 4] = jnp.broadcast_to(spread[0:64, 8 * j : 8 * j + 1], (64, 128))
        NS[j // 4, j % 4] = jnp.broadcast_to(spread[64:128, 8 * j : 8 * j + 1], (64, 128))
    head_here(0)
    take(0, 3)
    take(1, 1)
    send(1, 2)

    theirs, ours = 2 * (1 - t), 2 * t
    across = {"half": h, "vocab": v, "tok": 1 - t}

    def product(k, x0, n):
        X, W = sets[k][1], (WS, WT)[k]
        cols = pl.ds(pl.multiple_of(n * COLS, COLS), COLS)
        width = X.shape[-1]
        parts = [
            jnp.dot(X[c, pl.ds(x0, 2)].reshape(MINE, width), W[c, :, cols], preferred_element_type=f32)
            for c in (0, 1)
        ]
        return parts[0] + parts[1]

    def exchange(k, n):
        U, R = ((US, RS), (UT, RT))[k]
        return remote(U.at[n], R.at[n], e_send.at[k, n], e_recv.at[k, n], across)

    def theirs_tile(k, n):
        U, inv = (US, UT)[k], (NS, NT)[k]
        ACC[...] = product(k, theirs, n)

        def part(j, bounds):
            rows = pl.ds(pl.multiple_of(j * PART, PART), PART)
            value = ACC[rows, :] * jnp.concatenate([inv[theirs + j // 4, j % 4]] * (COLS // 128), axis=1)
            ACC[rows, :] = value
            size = jnp.max(jnp.abs(value), axis=1, keepdims=True)
            power = jnp.ceil(jnp.log2(jnp.maximum(size, 1e-30)) + 1e-4)
            STA[rows, :] = jnp.broadcast_to(power, (PART, 128))
            U[n, rows, :] = jnp.round(value * (jnp.exp2(-power) * FULL)).astype(jnp.int32).astype(i16)
            return bounds

        lax.fori_loop(0, MINE // PART, part, 0)
        U[n, pl.ds(MINE, 16), :] = jnp.transpose(STA[...])[0:16].astype(jnp.int32).astype(i16)

    def theirs_tiles(k):
        def tile(n, carry):
            theirs_tile(k, n)

            @pl.when(n > 0)
            def _():
                exchange(k, n - 1).start()

            return carry

        lax.fori_loop(0, TILES, tile, 0)

    def ours_tiles(k):
        O = (OS, OT)[k]

        def tile(n, carry):
            O[n] = product(k, ours, n)

            @pl.when(n == 0)
            def _():
                exchange(k, TILES - 1).start()

            return carry

        lax.fori_loop(0, TILES, tile, 0)

    theirs_tiles(0)
    ours_tiles(0)
    take(1, 2)
    send(1, 3)
    head_here(1)
    take(1, 3)
    theirs_tiles(1)
    ours_tiles(1)

    label = turned(jnp.broadcast_to(lab[...].astype(f32), (8, MINE))).astype(jnp.int32)
    FIN[...] = label.astype(f32)
    low = jnp.full((MINE, 128), -3.0e38, f32)
    none = jnp.zeros((MINE, 128), f32)
    MS[...] = low
    MT[...] = low
    for ref in (LS, TG, LT, CR):
        ref[...] = none

    def arrive(k, n):
        O, R, inv, M, L = ((OS, RS, NS, MS, LS), (OT, RT, NT, MT, LT))[k]
        exchange(k, n).wait_recv()
        head = R[n, pl.ds(MINE, 16), :].astype(jnp.int32).astype(f32)[0:8]
        STA[...] = turned(head)

        def part(j, carry):
            rows = pl.ds(pl.multiple_of(j * PART, PART), PART)
            scale = jnp.exp2(STA[rows, :]) * (1.0 / FULL)
            norm = inv[ours + j // 4, j % 4]
            groups = []
            for g in range(COLS // 128):
                cols = pl.ds(g * 128, 128)
                sent = R[n, rows, cols].astype(jnp.int32).astype(f32)
                groups.append(O[n, rows, cols] * norm + sent * scale)
                O[n, rows, cols] = groups[g]
            old = M[rows, :]
            new = old
            for value in groups:
                new = jnp.maximum(new, value)
            shrink = jnp.exp(old - new)
            sums = L[rows, :] * shrink
            if k == 1:
                cross = CR[rows, :] * shrink
            else:
                target = TG[rows, :]
                label = FIN[rows, :].astype(jnp.int32)
                base = v * WIDE + n * COLS + lax.broadcasted_iota(jnp.int32, (PART, 128), 1)
            for g, value in enumerate(groups):
                grown = jnp.exp(value - new)
                sums = sums + grown
                if k == 1:
                    cross = cross + grown * (value - OS[n, rows, pl.ds(g * 128, 128)])
                else:
                    target = target + jnp.where(base + g * 128 == label, value, 0.0)
            M[rows, :] = new
            L[rows, :] = sums
            if k == 1:
                CR[rows, :] = cross
            else:
                TG[rows, :] = target
            return carry

        lax.fori_loop(0, MINE // PART, part, 0)

    for k in (0, 1):
        def arrived_tile(n, carry, k=k):
            arrive(k, n)
            return carry

        lax.fori_loop(0, TILES, arrived_tile, 0)

    def lanes(j, carry):
        rows = pl.ds(pl.multiple_of(j * PART, PART), PART)
        m_t, m_s = MT[rows, :], MS[rows, :]
        t_max = jnp.max(m_t, axis=1, keepdims=True)
        s_max = jnp.max(m_s, axis=1, keepdims=True)
        w_t, w_s = jnp.exp(m_t - t_max), jnp.exp(m_s - s_max)
        columns = (
            t_max,
            jnp.sum(LT[rows, :] * w_t, axis=1, keepdims=True),
            jnp.sum(CR[rows, :] * w_t, axis=1, keepdims=True),
            s_max,
            jnp.sum(LS[rows, :] * w_s, axis=1, keepdims=True),
            jnp.sum(TG[rows, :], axis=1, keepdims=True),
        )
        lane = lax.broadcasted_iota(jnp.int32, (PART, 128), 1)
        packed = jnp.zeros((PART, 128), f32)
        for i, column in enumerate(columns):
            packed = jnp.where(lane == i, column, packed)
        STA[rows, :] = packed
        return carry

    lax.fori_loop(0, MINE // PART, lanes, 0)
    STR[0] = jnp.transpose(STA[...])[0:8]

    def meet(base, offsets, places, me, count):
        for i, where in enumerate(places):
            go(remote(STR.at[base], STR.at[base + 1 + i], s_send.at[base + i], s_recv.at[base + i], where))
        for i, where in enumerate(places):
            ref = STR.at[base + 1 + i]
            remote(ref, ref, s_send.at[base + i], s_recv.at[base + i], where).wait_recv()
        out = STR[base]
        for i in range(len(places)):
            out = joined(out, STR[base + 1 + i])
        return out

    STR[4] = meet(0, None, [at(x, z + d) for d in (1, 2, 3)], z, N)
    STR[8] = meet(4, None, [at(x + d, z) for d in (1, 2, 3)], x, N)
    whole = meet(8, None, [{"half": h, "vocab": far, "tok": t}], yh, 2)

    t_max, t_total, cross = whole[0:1], whole[1:2], whole[2:3]
    s_max, s_total, target = whole[3:4], whole[4:5], whole[5:6]
    student_lse = s_max + jnp.log(s_total)
    loss[...] = (
        cross / t_total - t_max - jnp.log(t_total) + student_lse + LABEL_WEIGHT * (student_lse - target)
    )
    factors = jnp.concatenate(
        [s_max, (1.0 + LABEL_WEIGHT) / s_total, t_max, 1.0 / t_total, jnp.zeros((124, MINE), f32)],
        axis=0,
    )
    STA[...] = jnp.transpose(factors)

    def results(j, carry):
        rows = pl.ds(pl.multiple_of(j * PART, PART), PART)
        per_row = STA[rows, :]
        m_s, c_s, m_t, c_t = (jnp.broadcast_to(per_row[:, i : i + 1], (PART, 128)) for i in range(4))
        label = FIN[rows, :].astype(jnp.int32)
        column = v * WIDE + lax.broadcasted_iota(jnp.int32, (PART, 128), 1)
        for n in range(TILES):
            for g in range(COLS // 128):
                cols = pl.ds(g * 128, 128)
                value = jnp.exp(OS[n, rows, cols] - m_s) * c_s - jnp.exp(OT[n, rows, cols] - m_t) * c_t
                here = column + (n * COLS + g * 128) == label
                value = value - jnp.where(here, LABEL_WEIGHT, 0.0)
                OUT[rows, pl.ds(n * COLS + g * 128, 128)] = value.astype(bf16)
        return carry

    lax.fori_loop(0, MINE // PART, results, 0)
    out = pltpu.make_async_copy(OUT, grad, o_sem)
    out.start()

    for copy in started:
        copy.wait_send()

    @pl.when(h != yh)
    def _():
        first(0, False).wait_send()
        squares_to(0, 0).wait_send()
        first(1, False).wait_send()

    for k in (0, 1):
        for n in range(TILES):
            exchange(k, n).wait_send()
    out.wait()


def shards(th, sh, gt, gs, wt, ws, labels):
    kt, ks = wt.shape[0], ws.shape[0]
    vmem = pl.BlockSpec(memory_space=pltpu.VMEM)
    hbm = pl.BlockSpec(memory_space=pl.ANY)
    dma = pltpu.SemaphoreType.DMA
    V = pltpu.VMEM
    scratch = [
        V((2, N, N, ROWS, ks), bf16), V((2, N, N, ROWS, kt), bf16),
        V((2, ks, WIDE), bf16), V((2, kt, WIDE), bf16),
        V((ROWS, ks), bf16), V((ROWS, kt), bf16),
        V((8, 128), f32), V((4, 8, 128), f32), V((N, N, 8, 128), f32),
        V((N, N, ROWS, 128), f32), V((N, N, ROWS, 128), f32),
        V((MINE, COLS), f32),
        V((TILES, MINE, COLS), f32), V((TILES, MINE, COLS), f32),
        V((TILES, MINE + 16, COLS), i16), V((TILES, MINE + 16, COLS), i16),
        V((TILES, MINE + 16, COLS), i16), V((TILES, MINE + 16, COLS), i16),
        V((MINE, WIDE), bf16),
        *[V((MINE, 128), f32) for _ in range(7)],
        V((10, 8, MINE), f32),
        V((MINE, 128), f32),
        dma((2, 2)), dma((2, 2)), dma((4,)), dma((4,)), dma((2, 3)), dma((2, 3)),
        dma((2,)), dma((2,)), dma((2,)),
        dma((2, 2, 8)), dma((2, 2, 8)), dma((2, TILES)), dma((2, TILES)), dma((10,)), dma((10,)),
        dma,
    ]
    loss, grad = pl.pallas_call(
        kernel,
        out_shape=(
            jax.ShapeDtypeStruct((1, MINE), f32),
            jax.ShapeDtypeStruct((MINE, WIDE), bf16),
        ),
        in_specs=[vmem] * 5 + [hbm] * 2,
        out_specs=(vmem, hbm),
        scratch_shapes=scratch,
        compiler_params=pltpu.CompilerParams(
            collective_id=0, has_side_effects=True, vmem_limit_bytes=67043328
        ),
    )(th, sh, gt.reshape(1, kt), gs.reshape(1, ks), labels.reshape(1, MINE), wt, ws)
    return loss.reshape(MINE), grad


def solution(mesh):
    return jax.shard_map(
        shards,
        mesh=mesh,
        in_specs=(
            P("vocab", ("half", "tok")),
            P("vocab", ("half", "tok")),
            P(("half", "tok")),
            P(("half", "tok")),
            P(("half", "tok"), "vocab"),
            P(("half", "tok"), "vocab"),
            P(("half", "tok")),
        ),
        out_specs=(P(("half", "tok")), P(("half", "tok"), "vocab")),
        check_vma=False,
    )
```

time: 645 us -> 164 us (0.25)
  waiting for transfers between devices: 525 us -> 0 us
  Pallas kernels: 0 us -> 159 us
  matrix products: 35.9 us -> 0 us
  other arithmetic: 35.3 us -> 0 us
  blocking collectives: 29.5 us -> 0 us
  between operations: 15.3 us -> 0.64 us
    reduce_scatter x3 -> x0, waiting for transfers between devices: 391 us -> none  [the longest x1 287 us: in_one_piece_2(): lax.psum_scatter(both, axis, scatter_dimension=dim, tiled=True)]
    pallas_call x0 -> x1, Pallas kernels: none -> 159 us  [shards(): pl.pallas_call(kernel, out_shape=(jax.ShapeDtypeStruct((1, MINE), f32), j...]
    all_gather x1 -> x0, waiting for transfers between devices: 134 us -> none  [in_one_piece(): out, at, done = (lax.all_gather(both, axis, axis=dim, tiled=True), 0, [])]
    dot_general x2 -> x0, matrix products: 35.9 us -> none  [the longest x1 24 us: shards(): jnp.dot(scaled_t, teacher_head, preferred_element_type=jnp.float32)]
    all_to_all x1 -> x0, blocking collectives: 22 us -> none  [sent_to_all(): return lax.all_to_all(copies, axis, split_axis=0, concat_axis=0, tiled=True)]
    reduce_sum x4 -> x0, other arithmetic: 13 us -> none  [the longest x2 8.16 us: prepare(): squares = jnp.sum(values * values, axis=1)]
    concatenate x2 -> x0, other arithmetic: 11.8 us -> none  [the longest x1 10 us: in_one_piece_2(): both = jnp.concatenate(columns, axis=along)]
    unnamed x2 -> x0, blocking collectives: 7.45 us -> none
  transfers between devices with their start and end apart: 4 -> 0, of which waited for: 4 -> 0; matrix products, arithmetic and copies ran while one was open for 5% -> 0% of each run, Pallas kernels for 0% -> 0%
where the time goes in v1:
time: 164 us
  Pallas kernels  159 us (97%)
  local copies, waits for them, and re-layouts  4.4 us (3%)
    pallas_call x1, Pallas kernels, shards(): pl.pallas_call(kernel, out_shape=(jax.ShapeDtypeStruct((1, MINE), f32), j...  159 us
    unnamed x2, local copies, waits for them, and re-layouts  4.4 us

profile of v1, /device:TPU:0, one launch (start us, length us, event | category | flops | bytes accessed | tf_op | source)
XLA Modules:
  0.0 164.1 jit_solution(15597962405364281522)
XLA Ops:
  0.6 159.1 %shard_map.86 = (f32[1,512]{1,0:T(1,128)}, bf16[512,2048]{1,0:T(8,128)(2,1)}) custom-call(bf16[64,2048]{1,0:T(8,128)(2,1)} %th.1, bf16[64,1024]{1,0:T(8,128)(2,1)} %sh.1, f32[1,2048]{1,0:T(1,128)} %bitcast.4, f32[1,1024]{1,0:T(1,128)} %bitcast.5, s32[1,512]{1,0:T(1,128)} %bitcast.6, bf16[2048,2048]{1,0:T(8,128)(2,1)} %wt.1, bf16[1024,2048]{1,0:T(8,128)(2,1)} %ws.1), custom_call_target="tpu_custom_call" | custom-call | tf_op jit(solution)/shard_map/pallas_call | solution.py:494
  159.7 1.2 copy.11
  161.0 3.2 %copy.12 = bf16[512,2048]{1,0:T(8,128)(2,1)} copy(bf16[512,2048]{1,0:T(8,128)(2,1)} %get-tuple-element.9) | data formatting | bytes 4194304
